TPU v7x, 32 devices: a whole 2x2x4 slice. The times are simulated.
32 devices in a mesh: region: 2 (over x), feat: 4 (over y, core), row: 4 (over z).
Axes of the slice: x: 2, y: 2, z: 4, core: 2. Of those that a mesh axis runs over, the one named last changes fastest.
Arguments:
- samples: bfloat16 [65536, 128], P(('region', 'row')), may hold values from -6 to 6
- targets: bfloat16 [65536, 64], P(('region', 'row')), may hold values from -6 to 6
- member: int32 [65536], P(('region', 'row')), may hold values 0 or 1
- omega: bfloat16 [128, 4096], P(None, 'feat'), may hold values from -0.5 to 0.5
- phase: float32 [4096], P('feat'), may hold values from -3.140625 to 3.140625
- factors: float32 [8192, 1024], P(('region', 'feat')), may hold values from -0.08 to 5, as said below
- weights_init: float32 [8192, 64], P(('region', 'feat'), 'row'), may hold values from -3 to 3
- duals_init: float32 [8192, 64], P(('region', 'feat'), 'row'), may hold values from -2 to 2
- consensus_init: float32 [4096, 64], P('feat', 'row'), may hold values from -3 to 3
- penalty_init: float32 [2], P('region'), may hold values from 2 to 8
Outputs:
- weights: float32 [8192, 64], P(('region', 'feat'), 'row')
- duals: float32 [8192, 64], P(('region', 'feat'), 'row')
- consensus: float32 [4096, 64], P('feat', 'row')
- penalty: float32 [2, 3], P('region')
Inputs may be any that keep to these rules, and one draw needn't show every extreme that they name: factors: each 1024 x 1024 block is lower triangular, its diagonal between 3.5 and 5, its entries below the diagonal drawn independently, symmetric about zero and at most 0.08 in magnitude.
All inputs are finite; a program needn't handle non-finite values. No bound on the sum of `member` on one device may be relied on, other than what follows from the above.
Results may differ from a plain program's by a relative error of at most 0.006.
Values may be sent and summed in bfloat16 or wider, within the bound.
A program may use at most 128 MiB of HBM per device.

v0:
```python
import functools
import math

import jax
import jax.numpy as jnp
from jax import lax
from jax.experimental import pallas as pl
from jax.experimental.pallas import tpu as pltpu
from jax.sharding import PartitionSpec as P

ITERS = 3
CORES = 2
PARTS = 2
MESH = pl.DeviceIdType.MESH
INV_TURN = 1.0 / (2.0 * math.pi)
COS_TERMS = (0.99999921, -19.73898042, 64.9286585, -85.2716283, 58.79050663, -21.07110846)
F32 = jnp.float32
BF16 = jnp.bfloat16


def dot(a, b):
    return lax.dot_general(a, b, (((1,), (0,)), ((), ())), preferred_element_type=F32)


def dot_nt(a, b):
    return lax.dot_general(a, b, (((1,), (1,)), ((), ())), preferred_element_type=F32)


def feature_tile(scale, omega, phase, samples):
    turns = dot_nt(omega, samples) * INV_TURN + phase * INV_TURN
    rest = turns - jnp.round(turns)
    square = rest * rest
    value = scale * COS_TERMS[-1]
    for term in COS_TERMS[-2::-1]:
        value = value * square + scale * term
    return value.astype(BF16)


def invert(base, factor_ref, dinv_ref, n_ref, t_ref):
    size = factor_ref.shape[0]
    t_ref[...] = jnp.zeros_like(t_ref)
    powers, totals = [], []
    for start in range(0, size, base):
        rows = factor_ref[start : start + base, :]
        row = lax.broadcasted_iota(jnp.int32, rows.shape, 0) + start
        column = lax.broadcasted_iota(jnp.int32, rows.shape, 1)
        diagonal = jnp.sum(jnp.where(row == column, rows, 0.0), axis=1, keepdims=True)
        n_ref[start : start + base, :] = jnp.where(row > column, rows / diagonal, 0.0).astype(BF16)
        block = factor_ref[start : start + base, start : start + base]
        inner_row = lax.broadcasted_iota(jnp.int32, block.shape, 0)
        inner_column = lax.broadcasted_iota(jnp.int32, block.shape, 1)
        on = jnp.sum(jnp.where(inner_row == inner_column, block, 0.0), axis=0, keepdims=True)
        dinv_ref[:, start : start + base] = 1.0 / on
        power = -n_ref[start : start + base, start : start + base].astype(F32)
        powers.append(power)
        totals.append(power)
    reach = 2
    while reach < base:
        for index in range(len(powers)):
            low = powers[index].astype(BF16)
            square = dot(low, low)
            low = square.astype(BF16)
            totals[index] = totals[index] + square + dot(totals[index].astype(BF16), low)
            powers[index] = square
        reach *= 2
    for index, start in enumerate(range(0, size, base)):
        t_ref[start : start + base, start : start + base] = totals[index].astype(BF16)
    width = base
    while width < size:
        for start in range(0, size, 2 * width):
            top = slice(start, start + width)
            bottom = slice(start + width, start + 2 * width)
            below = n_ref[bottom, top]
            first = below.astype(F32) + dot(below, t_ref[top, top])
            second = first + dot(t_ref[bottom, bottom], first.astype(BF16))
            t_ref[bottom, top] = (-second).astype(BF16)
        width *= 2


def admm_kernel(
    sizes,
    offset,
    scale,
    penalty_ref,
    samples_hbm,
    targets_hbm,
    member_hbm,
    omega_ref,
    phase_ref,
    factor_hbm,
    weights_ref,
    duals_ref,
    consensus_ref,
    out_ref,
    history_ref,
    factor_ref,
    dinv_ref,
    strict_ref,
    solve_ref,
    samples_ref,
    targets_ref,
    member_ref,
    far_omega_ref,
    far_phase_ref,
    turned_ref,
    column_ref,
    feat_ref,
    coarse_ref,
    acc_ref,
    part_ref,
    other_ref,
    resid_ref,
    gfar_ref,
    gside_ref,
    gsum_ref,
    gsend_ref,
    grow_ref,
    reg_ref,
    gap_ref,
    load_sem,
    omega_send,
    omega_recv,
    crow_send,
    crow_recv,
    cside_send,
    cside_recv,
    core_send,
    core_recv,
    gside_send,
    gside_recv,
    grow_send,
    grow_recv,
    reg_send,
    reg_recv,
    gap_send,
    gap_recv,
):
    n_region, n_feat, n_row = sizes
    narrow, width = weights_ref.shape
    outputs = n_row * narrow
    count = feat_ref.shape[2]
    chunk = min(1024, count)
    chunks = count // chunk
    piece_width = width // PARTS
    tile, broad = min(256, piece_width), min(512, piece_width)
    region, feat, row = lax.axis_index("region"), lax.axis_index("feat"), lax.axis_index("row")
    group = n_feat * n_row
    place = feat * n_row + row
    side = (region, lax.rem(feat + CORES, n_feat), row)
    core = (region, feat + 1 - 2 * lax.rem(feat, CORES), row)

    def row_peer(k):
        return (region, feat, lax.rem(row + k, n_row))

    def region_peer(k):
        return (lax.rem(region + k, n_region), feat, row)

    def group_peer(k):
        other = lax.rem(place + k, group)
        return (region, other // n_row, lax.rem(other, n_row))

    def remote(src, dst, send, recv, device):
        return pltpu.make_async_remote_copy(
            src_ref=src, dst_ref=dst, send_sem=send, recv_sem=recv,
            device_id=device, device_id_type=MESH,
        )

    first = pl.multiple_of((feat // CORES) * count, 128)
    span = pl.ds(first, count)
    loads = [
        pltpu.make_async_copy(samples_hbm.at[span], samples_ref, load_sem.at[0]),
        pltpu.make_async_copy(targets_hbm.at[:, span], targets_ref, load_sem.at[1]),
        pltpu.make_async_copy(member_hbm.at[:, span], member_ref, load_sem.at[2]),
        pltpu.make_async_copy(factor_hbm, factor_ref, load_sem.at[3]),
    ]
    for load in loads:
        load.start()

    barrier = pltpu.get_barrier_semaphore()
    for k in range(1, group):
        pl.semaphore_signal(barrier, inc=1, device_id=group_peer(k), device_id_type=MESH)
    for k in range(1, n_region):
        pl.semaphore_signal(barrier, inc=1, device_id=region_peer(k), device_id_type=MESH)

    trips = (width // tile) * chunks

    def prepare(omega, phase):
        turned_ref[...] = omega.astype(F32).T.astype(BF16)
        for j in range(width // tile):
            span = slice(j * tile, (j + 1) * tile)
            level = lax.broadcasted_iota(jnp.int32, (tile, tile), 0)
            across = lax.broadcasted_iota(jnp.int32, (tile, tile), 1)
            only = jnp.where(level == across, phase[:, span], 0.0)
            column_ref[span, :] = jnp.sum(only, axis=1, keepdims=True)

    def fill(half, low, high):
        def step(i, carry):
            down = pl.multiple_of((i // chunks) * tile, tile)
            right = pl.multiple_of((i % chunks) * chunk, chunk)
            feat_ref[half, pl.ds(down, tile), pl.ds(right, chunk)] = feature_tile(
                scale,
                turned_ref[pl.ds(down, tile), :],
                column_ref[pl.ds(down, tile), :],
                samples_ref[pl.ds(right, chunk), :],
            )
            return carry

        lax.fori_loop(low, high, step, 0)

    weights, duals, consensus = weights_ref[...], duals_ref[...], consensus_ref[...]
    rho = jnp.full((1, 128), penalty_ref[0], F32)
    history = jnp.zeros((1, 128), F32)
    lane = lax.broadcasted_iota(jnp.int32, (1, 128), 1)
    loads[0].wait()
    prepare(omega_ref[...], phase_ref[...])
    fill(0, 0, trips // 2)
    pl.semaphore_wait(barrier, group - 1 + n_region - 1)
    sends = []

    for t in range(ITERS):
        coarse_ref[t, 0, row] = weights.astype(BF16)
        mine = coarse_ref.at[t, 0, row]
        for k in range(1, n_row):
            copy = remote(mine, mine, crow_send.at[t, k], crow_recv.at[t, k], row_peer(k))
            copy.start()
            sends.append(copy)
        copy = remote(
            mine, coarse_ref.at[t, 1, row], cside_send.at[t, 0], cside_recv.at[t, 0], side
        )
        copy.start()
        sends.append(copy)

        if t > 0:
            duals, consensus = finish_region(t - 1)
        else:
            exchange = [
                remote(omega_ref, far_omega_ref, omega_send.at[0], omega_recv.at[0], side),
                remote(phase_ref, far_phase_ref, omega_send.at[1], omega_recv.at[1], side),
            ]
            for copy in exchange:
                copy.start()
                sends.append(copy)
            fill(0, trips // 2, trips)

        for k in range(1, n_row):
            source = lax.rem(row - k + n_row, n_row)
            piece = coarse_ref.at[t, 0, source]
            remote(piece, piece, crow_send.at[t, k], crow_recv.at[t, k], side).wait_recv()
            copy = remote(
                piece, coarse_ref.at[t, 1, source], cside_send.at[t, k], cside_recv.at[t, k], side
            )
            copy.start()
            sends.append(copy)
        if t == 0:
            for copy in exchange:
                copy.wait_recv()
            prepare(far_omega_ref[...], far_phase_ref[...])
            fill(1, 0, trips)
            loads[1].wait()
            loads[2].wait()
        near = coarse_ref[t, 0].reshape(outputs, width)
        for j in range(chunks):
            span = slice(j * chunk, (j + 1) * chunk)
            acc_ref[:, span] = dot(near, feat_ref[0, :, span])
        for k in range(n_row):
            source = lax.rem(row - k + n_row, n_row)
            piece = coarse_ref.at[t, 1, source]
            remote(piece, piece, cside_send.at[t, k], cside_recv.at[t, k], side).wait_recv()
        far = coarse_ref[t, 1].reshape(outputs, width)
        for j in range(chunks):
            span = slice(j * chunk, (j + 1) * chunk)
            part = acc_ref[:, span] + dot(far, feat_ref[1, :, span])
            acc_ref[:, span] = part
            part_ref[t, j] = part.astype(BF16)
            copy = remote(
                part_ref.at[t, j], other_ref.at[t, j], core_send.at[t, j], core_recv.at[t, j], core
            )
            copy.start()
            sends.append(copy)
        for j in range(chunks):
            span = slice(j * chunk, (j + 1) * chunk)
            piece = other_ref.at[t, j]
            remote(piece, piece, core_send.at[t, j], core_recv.at[t, j], core).wait_recv()
            predicted = acc_ref[:, span] + other_ref[t, j].astype(F32)
            gap_value = predicted - targets_ref[:, span].astype(F32)
            resid_ref[:, span] = (member_ref[:, span].astype(F32) * gap_value).astype(BF16)

        for p in range(PARTS):
            for j in range(piece_width // broad):
                inside = slice(j * broad, (j + 1) * broad)
                span = slice(p * piece_width + j * broad, p * piece_width + (j + 1) * broad)
                value = dot_nt(resid_ref[...], feat_ref[1, span, :])
                gfar_ref[t, p, :, :, inside] = value.astype(BF16).reshape(n_row, narrow, broad)
            copy = remote(
                gfar_ref.at[t, p], gside_ref.at[t, p], gside_send.at[t, p], gside_recv.at[t, p],
                side,
            )
            copy.start()
            sends.append(copy)
        for p in range(PARTS):
            for j in range(piece_width // broad):
                inside = slice(j * broad, (j + 1) * broad)
                span = slice(p * piece_width + j * broad, p * piece_width + (j + 1) * broad)
                value = dot_nt(resid_ref[...], feat_ref[0, span, :])
                gsum_ref[p, :, :, inside] = value.reshape(n_row, narrow, broad)
            piece = gside_ref.at[t, p]
            remote(piece, piece, gside_send.at[t, p], gside_recv.at[t, p], side).wait_recv()
            for k in range(1, n_row):
                target = lax.rem(row + k, n_row)
                value = gsum_ref[p, target] + gside_ref[t, p, target].astype(F32)
                gsend_ref[t, p, k] = value.astype(BF16)
                copy = remote(
                    gsend_ref.at[t, p, k], grow_ref.at[t, p, k], grow_send.at[t, p, k],
                    grow_recv.at[t, p, k], row_peer(k),
                )
                copy.start()
                sends.append(copy)
        if t > 0:
            rho, duals, history = finish_gap(t - 1, rho, duals, history)
        else:
            loads[3].wait()
            invert(min(256, width), factor_ref, dinv_ref, strict_ref, solve_ref)
        dinv = dinv_ref[...]
        scalar = rho[:, :1]
        gradient = []
        for p in range(PARTS):
            value = gsum_ref[p, row] + gside_ref[t, p, row].astype(F32)
            for k in range(1, n_row):
                piece = grow_ref.at[t, p, k]
                remote(
                    piece, piece, grow_send.at[t, p, k], grow_recv.at[t, p, k], side
                ).wait_recv()
                value = value + grow_ref[t, p, k].astype(F32)
            gradient.append(value)
        right = scalar * (weights - consensus + duals) + jnp.concatenate(gradient, axis=1)
        forward = right * dinv
        forward = forward + dot_nt(forward.astype(BF16), solve_ref[...])
        backward = (forward + dot(forward.astype(BF16), solve_ref[...])) * dinv
        weights = weights - backward

        reg_ref[t, region, :narrow] = scalar * (weights + duals)
        reg_ref[t, region, narrow:] = jnp.broadcast_to(scalar, (8, width))
        mine = reg_ref.at[t, region]
        for k in range(1, n_region):
            copy = remote(mine, mine, reg_send.at[t, k], reg_recv.at[t, k], region_peer(k))
            copy.start()
            sends.append(copy)

        def finish_region(s, weights=weights, duals=duals, consensus=consensus):
            for k in range(1, n_region):
                source = lax.rem(region - k + n_region, n_region)
                piece = reg_ref.at[s, source]
                remote(
                    piece, piece, reg_send.at[s, k], reg_recv.at[s, k], region_peer(k)
                ).wait_recv()
            total = reg_ref[s, 0]
            for r in range(1, n_region):
                total = total + reg_ref[s, r]
            updated = total[:narrow] / total[narrow : narrow + 1]
            gap = jnp.sum(jnp.square(weights - updated), keepdims=True).reshape(1, 1)
            drift = jnp.sum(jnp.square(updated - consensus), keepdims=True).reshape(1, 1)
            level = lax.broadcasted_iota(jnp.int32, (8, 128), 0)
            gap_ref[s, place] = jnp.where(level == 0, gap, drift)
            mine = gap_ref.at[s, place]
            for k in range(1, group):
                copy = remote(mine, mine, gap_send.at[s, k], gap_recv.at[s, k], group_peer(k))
                copy.start()
                sends.append(copy)
            return duals + weights - updated, updated

        def finish_gap(s, rho, duals, history):
            for k in range(1, group):
                source = lax.rem(place - k + group, group)
                piece = gap_ref.at[s, source]
                remote(
                    piece, piece, gap_send.at[s, k], gap_recv.at[s, k], group_peer(k)
                ).wait_recv()
            total = jnp.sum(gap_ref[s], axis=0)
            gap, drift = total[0:1], total[1:2]
            drift = rho * rho * drift
            renewed = rho * jnp.sqrt((gap + offset) / (drift + offset))
            duals = duals * (rho / renewed)[:, :1]
            return renewed, duals, jnp.where(lane == s, renewed, history)

    duals, consensus = finish_region(ITERS - 1)
    rho, duals, history = finish_gap(ITERS - 1, rho, duals, history)
    out_ref[0] = weights
    out_ref[1] = duals
    out_ref[2] = consensus
    history_ref[...] = history
    for copy in sends:
        copy.wait_send()


def admm(sizes, offset, scale, penalty, samples, targets, member, omega, phase, factors, *state):
    n_region, n_feat, n_row = sizes
    narrow, width = state[0].shape
    outputs = n_row * narrow
    inputs = omega.shape[0]
    count = samples.shape[0] // (n_feat // CORES)
    chunk = min(1024, count)
    chunks = count // chunk
    group = n_feat * n_row
    part = (n_row, narrow, width // PARTS)
    vmem = pl.BlockSpec(memory_space=pltpu.VMEM)
    hbm = pl.BlockSpec(memory_space=pl.ANY)
    dma = pltpu.SemaphoreType.DMA
    return pl.pallas_call(
        functools.partial(admm_kernel, sizes, offset, scale),
        in_specs=[pl.BlockSpec(memory_space=pltpu.SMEM), hbm, hbm, hbm] + [vmem, vmem, hbm, vmem, vmem, vmem],
        out_specs=[vmem, vmem],
        out_shape=[
            jax.ShapeDtypeStruct((3, narrow, width), F32),
            jax.ShapeDtypeStruct((1, 128), F32),
        ],
        scratch_shapes=[
            pltpu.VMEM((width, width), F32),
            pltpu.VMEM((1, width), F32),
            pltpu.VMEM((width, width), BF16),
            pltpu.VMEM((width, width), BF16),
            pltpu.VMEM((count, inputs), BF16),
            pltpu.VMEM((outputs, count), BF16),
            pltpu.VMEM((1, count), jnp.int32),
            pltpu.VMEM((inputs, width), BF16),
            pltpu.VMEM((1, width), F32),
            pltpu.VMEM((width, inputs), BF16),
            pltpu.VMEM((width, 1), F32),
            pltpu.VMEM((2, width, count), BF16),
            pltpu.VMEM((ITERS, 2, n_row, narrow, width), BF16),
            pltpu.VMEM((outputs, count), F32),
            pltpu.VMEM((ITERS, chunks, outputs, chunk), BF16),
            pltpu.VMEM((ITERS, chunks, outputs, chunk), BF16),
            pltpu.VMEM((outputs, count), BF16),
            pltpu.VMEM((ITERS, PARTS) + part, BF16),
            pltpu.VMEM((ITERS, PARTS) + part, BF16),
            pltpu.VMEM((PARTS,) + part, F32),
            pltpu.VMEM((ITERS, PARTS) + part, BF16),
            pltpu.VMEM((ITERS, PARTS) + part, BF16),
            pltpu.VMEM((ITERS, n_region, narrow + 8, width), F32),
            pltpu.VMEM((ITERS, group, 8, 128), F32),
            dma((4,)),
            dma((2,)),
            dma((2,)),
            dma((ITERS, n_row)),
            dma((ITERS, n_row)),
            dma((ITERS, n_row)),
            dma((ITERS, n_row)),
            dma((ITERS, chunks)),
            dma((ITERS, chunks)),
            dma((ITERS, PARTS)),
            dma((ITERS, PARTS)),
            dma((ITERS, PARTS, n_row)),
            dma((ITERS, PARTS, n_row)),
            dma((ITERS, n_region)),
            dma((ITERS, n_region)),
            dma((ITERS, group)),
            dma((ITERS, group)),
        ],
        compiler_params=pltpu.CompilerParams(
            collective_id=0, has_side_effects=True, vmem_limit_bytes=56 * 2**20
        ),
        name="admm",
    )(penalty, samples, targets, member, omega, phase, factors, *state)


def per_device(
    sizes,
    samples,
    targets,
    member,
    omega,
    phase,
    factors,
    weights_init,
    duals_init,
    consensus_init,
    penalty_init,
):
    n_region, n_feat, n_row = sizes
    total_features = n_feat * omega.shape[1]
    total_outputs = targets.shape[1]
    offset = 0.01 * total_features * total_outputs
    scale = math.sqrt(2.0 / total_features)
    final, history = admm(
        sizes, offset, scale, penalty_init, samples, targets.T, member[None, :], omega,
        phase[None, :], factors, weights_init.T, duals_init.T, consensus_init.T,
    )
    return (final[0].T, final[1].T, final[2].T, history[:, :ITERS])


def solution(mesh):
    sizes = (mesh.shape["region"], mesh.shape["feat"], mesh.shape["row"])
    return jax.shard_map(
        functools.partial(per_device, sizes),
        mesh=mesh,
        in_specs=(
            P(("region", "row"), None),
            P(("region", "row"), None),
            P(("region", "row")),
            P(None, "feat"),
            P("feat"),
            P(("region", "feat"), None),
            P(("region", "feat"), "row"),
            P(("region", "feat"), "row"),
            P("feat", "row"),
            P("region"),
        ),
        out_specs=(
            P(("region", "feat"), "row"),
            P(("region", "feat"), "row"),
            P("feat", "row"),
            P("region", None),
        ),
        check_vma=False,
    )
```

profile of v0, /device:TPU:0, one launch (start us, length us, event | category | flops | bytes accessed | tf_op | source)
XLA Modules:
  0.0 107.1 jit_solution(11627945754130548814)
XLA Ops:
  1.3 103.1 %admm.1 = (f32[3,16,1024]{2,1,0:T(8,128)}, f32[1,128]{1,0:T(1,128)}) custom-call(f32[1]{0:T(128)S(6)} %copy.15.penalty_ref, bf16[8192,128]{1,0:T(8,128)(2,1)} %samples_hbm.1, bf16[64,8192]{1,0:T(8,128)(2,1)} %bitcast.19, s32[1,8192]{1,0:T(1,128)} %bitcast.23, bf16[128,1024]{1,0:T(8,128)(2,1)} %omega_ref.1, f32[1,1024]{1,0:T(1,128)} %bitcast.24, ...), custom_call_target="tpu_custom_call" | custom-call | tf_op jit(solution)/shard_map/admm/pallas_call | solution.py:408
  104.4 1.6 %slice_bitcast_fusion = (f32[1024,16]{0,1:T(8,128)}, f32[1024,16]{0,1:T(8,128)}, f32[1024,16]{0,1:T(8,128)}) fusion(f32[3,16,1024]{2,1,0:T(8,128)} %get-tuple-element.6), kind=kLoop, calls=%fused_computation | loop fusion | bytes 393216 | tf_op jit(solution)/shard_map/transpose | solution.py:488
  106.0 1.1 %copy.16 = f32[1,3]{1,0:T(1,128)} copy(f32[1,3]{1,0:T(1,128)} %bitcast.25) | data formatting | bytes 24
where the time goes:
time: 107 us
  Pallas kernels  103 us (96%)
  local copies, waits for them, and re-layouts  2.7 us (3%)
  between operations  1.29 us (1%)
    pallas_call x1, Pallas kernels, admm(): pl.pallas_call(functools.partial(admm_kernel, sizes, offset, scale), in_s...  103 us

commit v1 on v0

--- a/solution.py
+++ b/solution.py
@@ -13,7 +13,8 @@
 PARTS = 2
 MESH = pl.DeviceIdType.MESH
 INV_TURN = 1.0 / (2.0 * math.pi)
-COS_TERMS = (0.99999921, -19.73898042, 64.9286585, -85.2716283, 58.79050663, -21.07110846)
+SINE_TERMS = (6.1875, -40.5, 72.5)
+SINE_GAIN = 1.0153050682891251
 F32 = jnp.float32
 BF16 = jnp.bfloat16
 
@@ -26,20 +27,18 @@
     return lax.dot_general(a, b, (((1,), (1,)), ((), ())), preferred_element_type=F32)
 
 
-def feature_tile(scale, omega, phase, samples):
-    turns = dot_nt(omega, samples) * INV_TURN + phase * INV_TURN
+def feature_tile(turns):
     rest = turns - jnp.round(turns)
-    square = rest * rest
-    value = scale * COS_TERMS[-1]
-    for term in COS_TERMS[-2::-1]:
-        value = value * square + scale * term
-    return value.astype(BF16)
-
-
-def invert(base, factor_ref, dinv_ref, n_ref, t_ref):
+    wave = (0.25 - jnp.abs(rest)).astype(BF16)
+    square = wave * wave
+    value = jnp.bfloat16(SINE_TERMS[-1])
+    for term in SINE_TERMS[-2::-1]:
+        value = value * square + jnp.bfloat16(term)
+    return wave * value
+
+
+def normalise(base, factor_ref, dinv_ref, n_ref):
     size = factor_ref.shape[0]
-    t_ref[...] = jnp.zeros_like(t_ref)
-    powers, totals = [], []
     for start in range(0, size, base):
         rows = factor_ref[start : start + base, :]
         row = lax.broadcasted_iota(jnp.int32, rows.shape, 0) + start
@@ -51,6 +50,13 @@
         inner_column = lax.broadcasted_iota(jnp.int32, block.shape, 1)
         on = jnp.sum(jnp.where(inner_row == inner_column, block, 0.0), axis=0, keepdims=True)
         dinv_ref[:, start : start + base] = 1.0 / on
+
+
+def invert(base, n_ref, t_ref):
+    size = n_ref.shape[0]
+    t_ref[...] = jnp.zeros_like(t_ref)
+    powers, totals = [], []
+    for start in range(0, size, base):
         power = -n_ref[start : start + base, start : start + base].astype(F32)
         powers.append(power)
         totals.append(power)
@@ -80,7 +86,7 @@
 def admm_kernel(
     sizes,
     offset,
-    scale,
+    gain,
     penalty_ref,
     samples_hbm,
     targets_hbm,
@@ -102,14 +108,16 @@
     member_ref,
     far_omega_ref,
     far_phase_ref,
-    turned_ref,
-    column_ref,
+    wave_ref,
+    twin_ref,
     feat_ref,
+    across_ref,
     coarse_ref,
     acc_ref,
     part_ref,
     other_ref,
     resid_ref,
+    total_ref,
     gfar_ref,
     gside_ref,
     gsum_ref,
@@ -142,7 +150,8 @@
     chunk = min(1024, count)
     chunks = count // chunk
     piece_width = width // PARTS
-    tile, broad = min(256, piece_width), min(512, piece_width)
+    tile = min(512, width)
+    inputs = samples_ref.shape[1]
     region, feat, row = lax.axis_index("region"), lax.axis_index("feat"), lax.axis_index("row")
     group = n_feat * n_row
     place = feat * n_row + row
@@ -182,40 +191,46 @@
     for k in range(1, n_region):
         pl.semaphore_signal(barrier, inc=1, device_id=region_peer(k), device_id_type=MESH)
 
-    trips = (width // tile) * chunks
-
-    def prepare(omega, phase):
-        turned_ref[...] = omega.astype(F32).T.astype(BF16)
-        for j in range(width // tile):
-            span = slice(j * tile, (j + 1) * tile)
-            level = lax.broadcasted_iota(jnp.int32, (tile, tile), 0)
-            across = lax.broadcasted_iota(jnp.int32, (tile, tile), 1)
-            only = jnp.where(level == across, phase[:, span], 0.0)
-            column_ref[span, :] = jnp.sum(only, axis=1, keepdims=True)
-
-    def fill(half, low, high):
+    def prepare(half, omega, phase):
+        exact = omega.astype(F32) * INV_TURN
+        high = exact.astype(BF16)
+        low = exact - high.astype(F32)
+        turn = phase * INV_TURN
+        first = turn.astype(BF16).astype(F32)
+        level = lax.broadcasted_iota(jnp.int32, low.shape, 0)
+        low = jnp.where(level == inputs - 2, first, jnp.where(level == inputs - 1, turn - first, low))
+        wave_ref[half, :, :inputs] = high.T
+        wave_ref[half, :, inputs:] = low.astype(BF16).T
+
+    def fill(half):
         def step(i, carry):
-            down = pl.multiple_of((i // chunks) * tile, tile)
-            right = pl.multiple_of((i % chunks) * chunk, chunk)
-            feat_ref[half, pl.ds(down, tile), pl.ds(right, chunk)] = feature_tile(
-                scale,
-                turned_ref[pl.ds(down, tile), :],
-                column_ref[pl.ds(down, tile), :],
-                samples_ref[pl.ds(right, chunk), :],
-            )
+            down = pl.multiple_of(i * tile, tile)
+            value = feature_tile(dot_nt(wave_ref[half, pl.ds(down, tile), :], twin_ref[...]))
+            feat_ref[half, pl.ds(down, tile), :] = value
+            across_ref[half, :, pl.ds(down, tile)] = value.T
             return carry
 
-        lax.fori_loop(low, high, step, 0)
+        lax.fori_loop(0, width // tile, step, 0)
 
     weights, duals, consensus = weights_ref[...], duals_ref[...], consensus_ref[...]
     rho = jnp.full((1, 128), penalty_ref[0], F32)
     history = jnp.zeros((1, 128), F32)
     lane = lax.broadcasted_iota(jnp.int32, (1, 128), 1)
+    prepare(0, omega_ref[...], phase_ref[...])
     loads[0].wait()
-    prepare(omega_ref[...], phase_ref[...])
-    fill(0, 0, trips // 2)
+    samples = samples_ref[...]
+    place_in = lax.broadcasted_iota(jnp.int32, samples.shape, 1)
+    twin_ref[:, :inputs] = samples
+    twin_ref[:, inputs:] = jnp.where(place_in < inputs - 2, samples.astype(F32), 1.0).astype(BF16)
     pl.semaphore_wait(barrier, group - 1 + n_region - 1)
     sends = []
+    exchange = [
+        remote(omega_ref, far_omega_ref, omega_send.at[0], omega_recv.at[0], side),
+        remote(phase_ref, far_phase_ref, omega_send.at[1], omega_recv.at[1], side),
+    ]
+    for copy in exchange:
+        copy.start()
+        sends.append(copy)
 
     for t in range(ITERS):
         coarse_ref[t, 0, row] = weights.astype(BF16)
@@ -229,18 +244,8 @@
         )
         copy.start()
         sends.append(copy)
-
-        if t > 0:
-            duals, consensus = finish_region(t - 1)
-        else:
-            exchange = [
-                remote(omega_ref, far_omega_ref, omega_send.at[0], omega_recv.at[0], side),
-                remote(phase_ref, far_phase_ref, omega_send.at[1], omega_recv.at[1], side),
-            ]
-            for copy in exchange:
-                copy.start()
-                sends.append(copy)
-            fill(0, trips // 2, trips)
+        if t == 0:
+            fill(0)
 
         for k in range(1, n_row):
             source = lax.rem(row - k + n_row, n_row)
@@ -251,17 +256,19 @@
             )
             copy.start()
             sends.append(copy)
-        if t == 0:
-            for copy in exchange:
-                copy.wait_recv()
-            prepare(far_omega_ref[...], far_phase_ref[...])
-            fill(1, 0, trips)
-            loads[1].wait()
-            loads[2].wait()
         near = coarse_ref[t, 0].reshape(outputs, width)
         for j in range(chunks):
             span = slice(j * chunk, (j + 1) * chunk)
             acc_ref[:, span] = dot(near, feat_ref[0, :, span])
+        if t > 0:
+            duals, consensus = finish_region(t - 1)
+        else:
+            for copy in exchange:
+                copy.wait_recv()
+            prepare(1, far_omega_ref[...], far_phase_ref[...])
+            fill(1)
+            loads[1].wait()
+            loads[2].wait()
         for k in range(n_row):
             source = lax.rem(row - k + n_row, n_row)
             piece = coarse_ref.at[t, 1, source]
@@ -281,16 +288,20 @@
             span = slice(j * chunk, (j + 1) * chunk)
             piece = other_ref.at[t, j]
             remote(piece, piece, core_send.at[t, j], core_recv.at[t, j], core).wait_recv()
-            predicted = acc_ref[:, span] + other_ref[t, j].astype(F32)
+            predicted = gain * (acc_ref[:, span] + other_ref[t, j].astype(F32))
             gap_value = predicted - targets_ref[:, span].astype(F32)
             resid_ref[:, span] = (member_ref[:, span].astype(F32) * gap_value).astype(BF16)
-
+            if j < chunks - 1:
+                value = dot(resid_ref[:, span], across_ref[1, span, :])
+                total_ref[...] = value if j == 0 else total_ref[...] + value
+
+        last = slice((chunks - 1) * chunk, chunks * chunk)
         for p in range(PARTS):
-            for j in range(piece_width // broad):
-                inside = slice(j * broad, (j + 1) * broad)
-                span = slice(p * piece_width + j * broad, p * piece_width + (j + 1) * broad)
-                value = dot_nt(resid_ref[...], feat_ref[1, span, :])
-                gfar_ref[t, p, :, :, inside] = value.astype(BF16).reshape(n_row, narrow, broad)
+            span = slice(p * piece_width, (p + 1) * piece_width)
+            value = dot(resid_ref[:, last], across_ref[1, last, span])
+            if chunks > 1:
+                value = value + total_ref[:, span]
+            gfar_ref[t, p] = value.astype(BF16).reshape(n_row, narrow, piece_width)
             copy = remote(
                 gfar_ref.at[t, p], gside_ref.at[t, p], gside_send.at[t, p], gside_recv.at[t, p],
                 side,
@@ -298,11 +309,13 @@
             copy.start()
             sends.append(copy)
         for p in range(PARTS):
-            for j in range(piece_width // broad):
-                inside = slice(j * broad, (j + 1) * broad)
-                span = slice(p * piece_width + j * broad, p * piece_width + (j + 1) * broad)
-                value = dot_nt(resid_ref[...], feat_ref[0, span, :])
-                gsum_ref[p, :, :, inside] = value.reshape(n_row, narrow, broad)
+            span = slice(p * piece_width, (p + 1) * piece_width)
+            value = dot(resid_ref[...], across_ref[0, :, span])
+            gsum_ref[p] = value.reshape(n_row, narrow, piece_width)
+        if t == 0:
+            loads[3].wait()
+            normalise(min(256, width), factor_ref, dinv_ref, strict_ref)
+        for p in range(PARTS):
             piece = gside_ref.at[t, p]
             remote(piece, piece, gside_send.at[t, p], gside_recv.at[t, p], side).wait_recv()
             for k in range(1, n_row):
@@ -318,8 +331,7 @@
         if t > 0:
             rho, duals, history = finish_gap(t - 1, rho, duals, history)
         else:
-            loads[3].wait()
-            invert(min(256, width), factor_ref, dinv_ref, strict_ref, solve_ref)
+            invert(min(256, width), strict_ref, solve_ref)
         dinv = dinv_ref[...]
         scalar = rho[:, :1]
         gradient = []
@@ -332,7 +344,7 @@
                 ).wait_recv()
                 value = value + grow_ref[t, p, k].astype(F32)
             gradient.append(value)
-        right = scalar * (weights - consensus + duals) + jnp.concatenate(gradient, axis=1)
+        right = scalar * (weights - consensus + duals) + gain * jnp.concatenate(gradient, axis=1)
         forward = right * dinv
         forward = forward + dot_nt(forward.astype(BF16), solve_ref[...])
         backward = (forward + dot(forward.astype(BF16), solve_ref[...])) * dinv
@@ -392,7 +404,7 @@
         copy.wait_send()
 
 
-def admm(sizes, offset, scale, penalty, samples, targets, member, omega, phase, factors, *state):
+def admm(sizes, offset, gain, penalty, samples, targets, member, omega, phase, factors, *state):
     n_region, n_feat, n_row = sizes
     narrow, width = state[0].shape
     outputs = n_row * narrow
@@ -406,7 +418,7 @@
     hbm = pl.BlockSpec(memory_space=pl.ANY)
     dma = pltpu.SemaphoreType.DMA
     return pl.pallas_call(
-        functools.partial(admm_kernel, sizes, offset, scale),
+        functools.partial(admm_kernel, sizes, offset, gain),
         in_specs=[pl.BlockSpec(memory_space=pltpu.SMEM), hbm, hbm, hbm] + [vmem, vmem, hbm, vmem, vmem, vmem],
         out_specs=[vmem, vmem],
         out_shape=[
@@ -423,14 +435,16 @@
             pltpu.VMEM((1, count), jnp.int32),
             pltpu.VMEM((inputs, width), BF16),
             pltpu.VMEM((1, width), F32),
-            pltpu.VMEM((width, inputs), BF16),
-            pltpu.VMEM((width, 1), F32),
+            pltpu.VMEM((2, width, 2 * inputs), BF16),
+            pltpu.VMEM((count, 2 * inputs), BF16),
             pltpu.VMEM((2, width, count), BF16),
+            pltpu.VMEM((2, count, width), BF16),
             pltpu.VMEM((ITERS, 2, n_row, narrow, width), BF16),
             pltpu.VMEM((outputs, count), F32),
             pltpu.VMEM((ITERS, chunks, outputs, chunk), BF16),
             pltpu.VMEM((ITERS, chunks, outputs, chunk), BF16),
             pltpu.VMEM((outputs, count), BF16),
+            pltpu.VMEM((outputs, width), F32),
             pltpu.VMEM((ITERS, PARTS) + part, BF16),
             pltpu.VMEM((ITERS, PARTS) + part, BF16),
             pltpu.VMEM((PARTS,) + part, F32),
@@ -457,7 +471,7 @@
             dma((ITERS, group)),
         ],
         compiler_params=pltpu.CompilerParams(
-            collective_id=0, has_side_effects=True, vmem_limit_bytes=56 * 2**20
+            collective_id=0, has_side_effects=True, vmem_limit_bytes=60 * 2**20
         ),
         name="admm",
     )(penalty, samples, targets, member, omega, phase, factors, *state)
@@ -480,9 +494,9 @@
     total_features = n_feat * omega.shape[1]
     total_outputs = targets.shape[1]
     offset = 0.01 * total_features * total_outputs
-    scale = math.sqrt(2.0 / total_features)
+    gain = SINE_GAIN * math.sqrt(2.0 / total_features)
     final, history = admm(
-        sizes, offset, scale, penalty_init, samples, targets.T, member[None, :], omega,
+        sizes, offset, gain, penalty_init, samples, targets.T, member[None, :], omega,
         phase[None, :], factors, weights_init.T, duals_init.T, consensus_init.T,
     )
     return (final[0].T, final[1].T, final[2].T, history[:, :ITERS])

time: 107 us -> 94.7 us (0.89)
  Pallas kernels: 103 us -> 90.5 us
    pallas_call x1, Pallas kernels: 103 us -> 90.5 us  [admm(): pl.pallas_call(functools.partial(admm_kernel, sizes, offset, gain), in_sp...]
where the time goes in v1:
time: 94.7 us; the launch traced here: 94.5 us
  Pallas kernels  90.5 us (96%)
  local copies, waits for them, and re-layouts  2.7 us (3%)
  between operations  1.29 us (1%)
    pallas_call x1, Pallas kernels, admm(): pl.pallas_call(functools.partial(admm_kernel, sizes, offset, gain), in_sp...  90.5 us

profile of v1, /device:TPU:0, one launch (start us, length us, event | category | flops | bytes accessed | tf_op | source)
XLA Modules:
  0.0 94.5 jit_solution(1771711745833818645)
XLA Ops:
  1.3 90.5 %admm.1 = (f32[3,16,1024]{2,1,0:T(8,128)}, f32[1,128]{1,0:T(1,128)}) custom-call(f32[1]{0:T(128)S(6)} %copy.15.penalty_ref, bf16[8192,128]{1,0:T(8,128)(2,1)} %samples_hbm.1, bf16[64,8192]{1,0:T(8,128)(2,1)} %bitcast.19, s32[1,8192]{1,0:T(1,128)} %bitcast.23, bf16[128,1024]{1,0:T(8,128)(2,1)} %omega_ref.1, f32[1,1024]{1,0:T(1,128)} %bitcast.24, ...), custom_call_target="tpu_custom_call" | custom-call | tf_op jit(solution)/shard_map/admm/pallas_call | solution.py:420
  91.8 1.6 %slice_bitcast_fusion = (f32[1024,16]{0,1:T(8,128)}, f32[1024,16]{0,1:T(8,128)}, f32[1024,16]{0,1:T(8,128)}) fusion(f32[3,16,1024]{2,1,0:T(8,128)} %get-tuple-element.6), kind=kLoop, calls=%fused_computation | loop fusion | bytes 393216 | tf_op jit(solution)/shard_map/transpose | solution.py:502
  93.4 1.1 %copy.16 = f32[1,3]{1,0:T(1,128)} copy(f32[1,3]{1,0:T(1,128)} %bitcast.25) | data formatting | bytes 24

commit v2 on v1

--- a/solution.py
+++ b/solution.py
@@ -91,14 +91,17 @@
     samples_hbm,
     targets_hbm,
     member_hbm,
+    omega_hbm,
+    phase_hbm,
+    factor_hbm,
+    weights_hbm,
+    duals_hbm,
+    consensus_hbm,
+    out_ref,
+    history_ref,
     omega_ref,
     phase_ref,
-    factor_hbm,
-    weights_ref,
-    duals_ref,
-    consensus_ref,
-    out_ref,
-    history_ref,
+    state_ref,
     factor_ref,
     dinv_ref,
     strict_ref,
@@ -144,7 +147,7 @@
     gap_recv,
 ):
     n_region, n_feat, n_row = sizes
-    narrow, width = weights_ref.shape
+    narrow, width = weights_hbm.shape
     outputs = n_row * narrow
     count = feat_ref.shape[2]
     chunk = min(1024, count)
@@ -153,9 +156,12 @@
     tile = min(512, width)
     inputs = samples_ref.shape[1]
     region, feat, row = lax.axis_index("region"), lax.axis_index("feat"), lax.axis_index("row")
+    outward = sorted(range(1, n_row), key=lambda k: -min(k, n_row - k))
+    inward = outward[::-1]
     group = n_feat * n_row
     place = feat * n_row + row
-    side = (region, lax.rem(feat + CORES, n_feat), row)
+    across_feat = lax.rem(feat + CORES, n_feat)
+    side = (region, across_feat + 1 - 2 * lax.rem(across_feat, CORES), row)
     core = (region, feat + 1 - 2 * lax.rem(feat, CORES), row)
 
     def row_peer(k):
@@ -181,9 +187,14 @@
         pltpu.make_async_copy(targets_hbm.at[:, span], targets_ref, load_sem.at[1]),
         pltpu.make_async_copy(member_hbm.at[:, span], member_ref, load_sem.at[2]),
         pltpu.make_async_copy(factor_hbm, factor_ref, load_sem.at[3]),
+        pltpu.make_async_copy(omega_hbm, omega_ref, load_sem.at[4]),
+        pltpu.make_async_copy(phase_hbm, phase_ref, load_sem.at[5]),
+        pltpu.make_async_copy(weights_hbm, state_ref.at[0], load_sem.at[6]),
+        pltpu.make_async_copy(duals_hbm, state_ref.at[1], load_sem.at[7]),
+        pltpu.make_async_copy(consensus_hbm, state_ref.at[2], load_sem.at[8]),
     ]
-    for load in loads:
-        load.start()
+    for index in (4, 5, 0, 6, 7, 8, 1, 2, 3):
+        loads[index].start()
 
     barrier = pltpu.get_barrier_semaphore()
     for k in range(1, group):
@@ -212,16 +223,20 @@
 
         lax.fori_loop(0, width // tile, step, 0)
 
-    weights, duals, consensus = weights_ref[...], duals_ref[...], consensus_ref[...]
     rho = jnp.full((1, 128), penalty_ref[0], F32)
     history = jnp.zeros((1, 128), F32)
     lane = lax.broadcasted_iota(jnp.int32, (1, 128), 1)
+    loads[4].wait()
+    loads[5].wait()
     prepare(0, omega_ref[...], phase_ref[...])
     loads[0].wait()
     samples = samples_ref[...]
     place_in = lax.broadcasted_iota(jnp.int32, samples.shape, 1)
     twin_ref[:, :inputs] = samples
     twin_ref[:, inputs:] = jnp.where(place_in < inputs - 2, samples.astype(F32), 1.0).astype(BF16)
+    for index in (6, 7, 8):
+        loads[index].wait()
+    weights, duals, consensus = state_ref[0], state_ref[1], state_ref[2]
     pl.semaphore_wait(barrier, group - 1 + n_region - 1)
     sends = []
     exchange = [
@@ -235,7 +250,7 @@
     for t in range(ITERS):
         coarse_ref[t, 0, row] = weights.astype(BF16)
         mine = coarse_ref.at[t, 0, row]
-        for k in range(1, n_row):
+        for k in outward:
             copy = remote(mine, mine, crow_send.at[t, k], crow_recv.at[t, k], row_peer(k))
             copy.start()
             sends.append(copy)
@@ -247,7 +262,7 @@
         if t == 0:
             fill(0)
 
-        for k in range(1, n_row):
+        for k in inward:
             source = lax.rem(row - k + n_row, n_row)
             piece = coarse_ref.at[t, 0, source]
             remote(piece, piece, crow_send.at[t, k], crow_recv.at[t, k], side).wait_recv()
@@ -318,7 +333,7 @@
         for p in range(PARTS):
             piece = gside_ref.at[t, p]
             remote(piece, piece, gside_send.at[t, p], gside_recv.at[t, p], side).wait_recv()
-            for k in range(1, n_row):
+            for k in outward:
                 target = lax.rem(row + k, n_row)
                 value = gsum_ref[p, target] + gside_ref[t, p, target].astype(F32)
                 gsend_ref[t, p, k] = value.astype(BF16)
@@ -419,13 +434,16 @@
     dma = pltpu.SemaphoreType.DMA
     return pl.pallas_call(
         functools.partial(admm_kernel, sizes, offset, gain),
-        in_specs=[pl.BlockSpec(memory_space=pltpu.SMEM), hbm, hbm, hbm] + [vmem, vmem, hbm, vmem, vmem, vmem],
+        in_specs=[pl.BlockSpec(memory_space=pltpu.SMEM), ] + [hbm] * 9,
         out_specs=[vmem, vmem],
         out_shape=[
-            jax.ShapeDtypeStruct((3, narrow, width), F32),
-            jax.ShapeDtypeStruct((1, 128), F32),
+            pltpu.VMEM((3, narrow, width), F32),
+            pltpu.VMEM((1, 128), F32),
         ],
         scratch_shapes=[
+            pltpu.VMEM((inputs, width), BF16),
+            pltpu.VMEM((1, width), F32),
+            pltpu.VMEM((3, narrow, width), F32),
             pltpu.VMEM((width, width), F32),
             pltpu.VMEM((1, width), F32),
             pltpu.VMEM((width, width), BF16),
@@ -452,7 +470,7 @@
             pltpu.VMEM((ITERS, PARTS) + part, BF16),
             pltpu.VMEM((ITERS, n_region, narrow + 8, width), F32),
             pltpu.VMEM((ITERS, group, 8, 128), F32),
-            dma((4,)),
+            dma((9,)),
             dma((2,)),
             dma((2,)),
             dma((ITERS, n_row)),

time: 94.7 us -> 90.2 us (0.952)
  Pallas kernels: 90.5 us -> 87.6 us
  local copies, waits for them, and re-layouts: 2.7 us -> 1.19 us
    pallas_call x1, Pallas kernels: 90.5 us -> 87.6 us  [admm(): pl.pallas_call(functools.partial(admm_kernel, sizes, offset, gain), in_sp...]
where the time goes in v2:
time: 90.2 us; the launch traced here: 90.1 us
  Pallas kernels  87.6 us (97%)
  between operations  1.29 us (1%)
  local copies, waits for them, and re-layouts  1.19 us (1%)
    pallas_call x1, Pallas kernels, admm(): pl.pallas_call(functools.partial(admm_kernel, sizes, offset, gain), in_sp...  87.6 us

profile of v2, /device:TPU:0, one launch (start us, length us, event | category | flops | bytes accessed | tf_op | source)
XLA Modules:
  0.0 90.1 jit_solution(6921807840292926554)
XLA Ops:
  1.3 87.6 %admm.1 = (f32[3,16,1024]{2,1,0:T(8,128)S(1)}, f32[1,128]{1,0:T(1,128)S(1)}) custom-call(f32[1]{0:T(128)S(6)} %copy.15.penalty_ref, bf16[8192,128]{1,0:T(8,128)(2,1)} %samples_hbm.1, bf16[64,8192]{1,0:T(8,128)(2,1)} %bitcast.20, s32[1,8192]{1,0:T(1,128)} %bitcast.24, bf16[128,1024]{1,0:T(8,128)(2,1)} %omega_hbm.1, f32[1,1024]{1,0:T(1,128)} %bitcast.25, ...), custom_call_target="tpu_custom_call" | custom-call | tf_op jit(solution)/shard_map/admm/pallas_call | solution.py:435
  88.9 0.7 slice_bitcast_fusion
  89.6 0.5 copy.16

commit v3 on v2

--- a/solution.py
+++ b/solution.py
@@ -150,10 +150,10 @@
     narrow, width = weights_hbm.shape
     outputs = n_row * narrow
     count = feat_ref.shape[2]
-    chunk = min(1024, count)
+    chunk = min(2048, count)
     chunks = count // chunk
     piece_width = width // PARTS
-    tile = min(512, width)
+    tile, base = min(512, width), min(256, width)
     inputs = samples_ref.shape[1]
     region, feat, row = lax.axis_index("region"), lax.axis_index("feat"), lax.axis_index("row")
     outward = sorted(range(1, n_row), key=lambda k: -min(k, n_row - k))
@@ -161,11 +161,15 @@
     group = n_feat * n_row
     place = feat * n_row + row
     across_feat = lax.rem(feat + CORES, n_feat)
-    side = (region, across_feat + 1 - 2 * lax.rem(across_feat, CORES), row)
+    side_feat = across_feat + 1 - 2 * lax.rem(across_feat, CORES)
+    side = (region, side_feat, row)
     core = (region, feat + 1 - 2 * lax.rem(feat, CORES), row)
 
     def row_peer(k):
         return (region, feat, lax.rem(row + k, n_row))
+
+    def side_peer(k):
+        return (region, side_feat, lax.rem(row + k, n_row))
 
     def region_peer(k):
         return (lax.rem(region + k, n_region), feat, row)
@@ -228,6 +232,15 @@
     lane = lax.broadcasted_iota(jnp.int32, (1, 128), 1)
     loads[4].wait()
     loads[5].wait()
+    pl.semaphore_wait(barrier, group - 1 + n_region - 1)
+    sends = []
+    exchange = [
+        remote(omega_ref, far_omega_ref, omega_send.at[0], omega_recv.at[0], side),
+        remote(phase_ref, far_phase_ref, omega_send.at[1], omega_recv.at[1], side),
+    ]
+    for copy in exchange:
+        copy.start()
+        sends.append(copy)
     prepare(0, omega_ref[...], phase_ref[...])
     loads[0].wait()
     samples = samples_ref[...]
@@ -237,15 +250,6 @@
     for index in (6, 7, 8):
         loads[index].wait()
     weights, duals, consensus = state_ref[0], state_ref[1], state_ref[2]
-    pl.semaphore_wait(barrier, group - 1 + n_region - 1)
-    sends = []
-    exchange = [
-        remote(omega_ref, far_omega_ref, omega_send.at[0], omega_recv.at[0], side),
-        remote(phase_ref, far_phase_ref, omega_send.at[1], omega_recv.at[1], side),
-    ]
-    for copy in exchange:
-        copy.start()
-        sends.append(copy)
 
     for t in range(ITERS):
         coarse_ref[t, 0, row] = weights.astype(BF16)
@@ -254,30 +258,25 @@
             copy = remote(mine, mine, crow_send.at[t, k], crow_recv.at[t, k], row_peer(k))
             copy.start()
             sends.append(copy)
-        copy = remote(
-            mine, coarse_ref.at[t, 1, row], cside_send.at[t, 0], cside_recv.at[t, 0], side
-        )
-        copy.start()
-        sends.append(copy)
         if t == 0:
             fill(0)
+        for k in outward + [0]:
+            copy = remote(
+                mine, coarse_ref.at[t, 1, row], cside_send.at[t, k], cside_recv.at[t, k],
+                side_peer(k),
+            )
+            copy.start()
+            sends.append(copy)
 
         for k in inward:
             source = lax.rem(row - k + n_row, n_row)
             piece = coarse_ref.at[t, 0, source]
             remote(piece, piece, crow_send.at[t, k], crow_recv.at[t, k], side).wait_recv()
-            copy = remote(
-                piece, coarse_ref.at[t, 1, source], cside_send.at[t, k], cside_recv.at[t, k], side
-            )
-            copy.start()
-            sends.append(copy)
         near = coarse_ref[t, 0].reshape(outputs, width)
         for j in range(chunks):
             span = slice(j * chunk, (j + 1) * chunk)
             acc_ref[:, span] = dot(near, feat_ref[0, :, span])
-        if t > 0:
-            duals, consensus = finish_region(t - 1)
-        else:
+        if t == 0:
             for copy in exchange:
                 copy.wait_recv()
             prepare(1, far_omega_ref[...], far_phase_ref[...])
@@ -299,6 +298,8 @@
             )
             copy.start()
             sends.append(copy)
+        if t > 0:
+            duals, consensus = finish_region(t - 1)
         for j in range(chunks):
             span = slice(j * chunk, (j + 1) * chunk)
             piece = other_ref.at[t, j]
@@ -317,41 +318,45 @@
             if chunks > 1:
                 value = value + total_ref[:, span]
             gfar_ref[t, p] = value.astype(BF16).reshape(n_row, narrow, piece_width)
-            copy = remote(
-                gfar_ref.at[t, p], gside_ref.at[t, p], gside_send.at[t, p], gside_recv.at[t, p],
-                side,
-            )
-            copy.start()
-            sends.append(copy)
+            for k in outward + [0]:
+                target = lax.rem(row + k, n_row)
+                copy = remote(
+                    gfar_ref.at[t, p, target], gside_ref.at[t, p, k], gside_send.at[t, p, k],
+                    gside_recv.at[t, p, k], side_peer(k),
+                )
+                copy.start()
+                sends.append(copy)
         for p in range(PARTS):
             span = slice(p * piece_width, (p + 1) * piece_width)
             value = dot(resid_ref[...], across_ref[0, :, span])
             gsum_ref[p] = value.reshape(n_row, narrow, piece_width)
-        if t == 0:
-            loads[3].wait()
-            normalise(min(256, width), factor_ref, dinv_ref, strict_ref)
-        for p in range(PARTS):
-            piece = gside_ref.at[t, p]
-            remote(piece, piece, gside_send.at[t, p], gside_recv.at[t, p], side).wait_recv()
+            gsend_ref[t, p] = value.astype(BF16).reshape(n_row, narrow, piece_width)
             for k in outward:
                 target = lax.rem(row + k, n_row)
-                value = gsum_ref[p, target] + gside_ref[t, p, target].astype(F32)
-                gsend_ref[t, p, k] = value.astype(BF16)
                 copy = remote(
-                    gsend_ref.at[t, p, k], grow_ref.at[t, p, k], grow_send.at[t, p, k],
+                    gsend_ref.at[t, p, target], grow_ref.at[t, p, k], grow_send.at[t, p, k],
                     grow_recv.at[t, p, k], row_peer(k),
                 )
                 copy.start()
                 sends.append(copy)
+        if t == 0:
+            loads[3].wait()
+            normalise(base, factor_ref, dinv_ref, strict_ref)
         if t > 0:
             rho, duals, history = finish_gap(t - 1, rho, duals, history)
         else:
-            invert(min(256, width), strict_ref, solve_ref)
+            invert(base, strict_ref, solve_ref)
         dinv = dinv_ref[...]
         scalar = rho[:, :1]
         gradient = []
         for p in range(PARTS):
-            value = gsum_ref[p, row] + gside_ref[t, p, row].astype(F32)
+            value = gsum_ref[p, row]
+            for k in range(n_row):
+                piece = gside_ref.at[t, p, k]
+                remote(
+                    piece, piece, gside_send.at[t, p, k], gside_recv.at[t, p, k], side
+                ).wait_recv()
+                value = value + gside_ref[t, p, k].astype(F32)
             for k in range(1, n_row):
                 piece = grow_ref.at[t, p, k]
                 remote(
@@ -361,8 +366,18 @@
             gradient.append(value)
         right = scalar * (weights - consensus + duals) + gain * jnp.concatenate(gradient, axis=1)
         forward = right * dinv
-        forward = forward + dot_nt(forward.astype(BF16), solve_ref[...])
-        backward = (forward + dot(forward.astype(BF16), solve_ref[...])) * dinv
+        low = forward.astype(BF16)
+        steps = [
+            dot_nt(low[:, : start + base], solve_ref[start : start + base, : start + base])
+            for start in range(0, width, base)
+        ]
+        forward = forward + jnp.concatenate(steps, axis=1)
+        low = forward.astype(BF16)
+        steps = [
+            dot(low[:, start:], solve_ref[start:, start : start + base])
+            for start in range(0, width, base)
+        ]
+        backward = (forward + jnp.concatenate(steps, axis=1)) * dinv
         weights = weights - backward
 
         reg_ref[t, region, :narrow] = scalar * (weights + duals)
@@ -425,7 +440,7 @@
     outputs = n_row * narrow
     inputs = omega.shape[0]
     count = samples.shape[0] // (n_feat // CORES)
-    chunk = min(1024, count)
+    chunk = min(2048, count)
     chunks = count // chunk
     group = n_feat * n_row
     part = (n_row, narrow, width // PARTS)
@@ -479,8 +494,8 @@
             dma((ITERS, n_row)),
             dma((ITERS, chunks)),
             dma((ITERS, chunks)),
-            dma((ITERS, PARTS)),
-            dma((ITERS, PARTS)),
+            dma((ITERS, PARTS, n_row)),
+            dma((ITERS, PARTS, n_row)),
             dma((ITERS, PARTS, n_row)),
             dma((ITERS, PARTS, n_row)),
             dma((ITERS, n_region)),

time: 90.2 us -> 85.3 us (0.946)
  Pallas kernels: 87.6 us -> 82.7 us
    pallas_call x1, Pallas kernels: 87.6 us -> 82.7 us  [admm(): pl.pallas_call(functools.partial(admm_kernel, sizes, offset, gain), in_sp...]
where the time goes in v3:
time: 85.3 us; the launch traced here: 85.2 us
  Pallas kernels  82.7 us (97%)
  between operations  1.29 us (2%)
  local copies, waits for them, and re-layouts  1.19 us (1%)
    pallas_call x1, Pallas kernels, admm(): pl.pallas_call(functools.partial(admm_kernel, sizes, offset, gain), in_sp...  82.7 us

profile of v3, /device:TPU:0, one launch (start us, length us, event | category | flops | bytes accessed | tf_op | source)
XLA Modules:
  0.0 85.2 jit_solution(9492656011926207062)
XLA Ops:
  1.3 82.7 %admm.1 = (f32[3,16,1024]{2,1,0:T(8,128)S(1)}, f32[1,128]{1,0:T(1,128)S(1)}) custom-call(f32[1]{0:T(128)S(6)} %copy.15.penalty_ref, bf16[8192,128]{1,0:T(8,128)(2,1)} %samples_hbm.1, bf16[64,8192]{1,0:T(8,128)(2,1)} %bitcast.20, s32[1,8192]{1,0:T(1,128)} %bitcast.24, bf16[128,1024]{1,0:T(8,128)(2,1)} %omega_hbm.1, f32[1,1024]{1,0:T(1,128)} %bitcast.25, ...), custom_call_target="tpu_custom_call" | custom-call | tf_op jit(solution)/shard_map/admm/pallas_call | solution.py:450
  84.0 0.7 slice_bitcast_fusion
  84.7 0.5 copy.16
